TPU v7x, 32 devices: a whole 2x2x4 slice. The times are simulated.
32 devices in a mesh: dp: 4 (over x, core), fsdp: 2 (over y), tensor: 4 (over z).
Axes of the slice: x: 2, y: 2, z: 4, core: 2. Of those that a mesh axis runs over, the one named last changes fastest.
Arguments:
- tokens: bfloat16 [8, 768, 8192], P(('dp', 'fsdp'), 'tensor'), may hold values from -6 to 6
- norm_gain: float32 [8192], replicated, may hold values from 0.85 to 4
- w_qkv: bfloat16 [8192, 5120], P(('dp', 'fsdp'), 'tensor'), may hold values from -0.3 to 0.3
- a_query: bfloat16 [8192, 16], replicated, may hold values from -0.0625 to 0.0625
- query_up_adapter: bfloat16 [16, 4096], P(None, 'tensor'), may hold values from -1.5 to 1.5
- a_value: bfloat16 [8192, 16], replicated, may hold values from -0.0625 to 0.0625
- value_up_adapter: bfloat16 [16, 512], P(None, 'tensor'), may hold values from -1.5 to 1.5
- out_grad: bfloat16 [8, 768, 4096], P(('dp', 'fsdp'), 'tensor'), may hold values from -6 to 6
Outputs:
- attn_out: bfloat16 [8, 768, 4096], P(('dp', 'fsdp'), 'tensor')
- grad_a_query: float32 [8192, 16], replicated
- grad_b_query: float32 [16, 4096], P(None, 'tensor')
- grad_a_value: float32 [8192, 16], replicated
- grad_b_value: float32 [16, 512], P(None, 'tensor')
All inputs are finite; a program needn't handle non-finite values.
Results may differ from a plain program's by a relative error of at most 0.015.
The roundings to bfloat16 on the way count: a program that leaves them out, or rounds other values in their place, can miss the bound.
Values may be sent and summed in bfloat16 or wider, within the bound.
A program may use at most 256 MiB of HBM per device.

v0:
```python
import math
import jax
import jax.numpy as jnp
from jax import lax
from jax.sharding import PartitionSpec as P

HD = 128
QUERY_PER_KV = 8
EPSILON = 1e-05
ADAPTER_SCALE = 2.0
ROPE_BASE = 500000.0


def normalize(own_rows, norm_gain):
    widened = own_rows.astype(jnp.float32)
    mean_square = jnp.mean(widened * widened, axis=-1, keepdims=True)
    return (widened * lax.rsqrt(mean_square + EPSILON) * norm_gain).astype(jnp.bfloat16)


def rotary(heads_block):
    sequence_length = heads_block.shape[0]
    half_dim = heads_block.shape[-1] // 2
    positions = jnp.arange(sequence_length, dtype=jnp.float32)[:, None]
    inv_freq = ROPE_BASE ** (-jnp.arange(half_dim, dtype=jnp.float32) / half_dim)
    angles = positions * inv_freq
    cosine = jnp.cos(angles)[:, None, :]
    sine_table = jnp.sin(angles)[:, None, :]
    front_half = heads_block[..., :half_dim].astype(jnp.float32)
    back_half = heads_block[..., half_dim:].astype(jnp.float32)
    turned = jnp.concatenate(
        [
            front_half * cosine - back_half * sine_table,
            back_half * cosine + front_half * sine_table,
        ],
        -1,
    )
    return turned.astype(jnp.bfloat16)


def attend(query_rows, key_heads, value_rows):
    sequence_length = query_rows.shape[0]
    kv_heads = key_heads.shape[1] // HD
    rot_queries = rotary(query_rows.reshape(sequence_length, kv_heads * QUERY_PER_KV, HD))
    rot_keys = rotary(key_heads.reshape(sequence_length, kv_heads, HD))
    split_values = value_rows.reshape(sequence_length, kv_heads, HD)
    causal = jnp.arange(sequence_length)[:, None] >= jnp.arange(sequence_length)[None, :]

    def one_head(head_index):
        q_head = lax.dynamic_index_in_dim(rot_queries, head_index, 1, keepdims=False)
        k_head = lax.dynamic_index_in_dim(rot_keys, head_index // QUERY_PER_KV, 1, keepdims=False)
        v_head = lax.dynamic_index_in_dim(
            split_values, head_index // QUERY_PER_KV, 1, keepdims=False
        )
        scores = jnp.dot(q_head, k_head.T, preferred_element_type=jnp.float32) * (
            1.0 / math.sqrt(HD)
        )
        scores = jnp.where(causal, scores, -1e30)
        row_max = jnp.max(scores, axis=-1, keepdims=True)
        weights = jnp.exp(scores - row_max)
        probabilities = (weights / jnp.sum(weights, axis=-1, keepdims=True)).astype(jnp.bfloat16)
        return jnp.dot(probabilities, v_head, preferred_element_type=jnp.float32).astype(
            jnp.bfloat16
        )

    per_head = lax.map(one_head, jnp.arange(kv_heads * QUERY_PER_KV, dtype=jnp.int32))
    return jnp.transpose(per_head, (1, 0, 2)).reshape(sequence_length, kv_heads * QUERY_PER_KV * HD)


def local(tokens, norm_gain, w_qkv, a_query, query_up_adapter, a_value, value_up_adapter, out_grad):
    normed_input = normalize(tokens[0], norm_gain)
    gathered = lax.all_gather(normed_input, "tensor", axis=0, tiled=True)
    sequence_length = gathered.shape[0]
    col_count = w_qkv.shape[1]
    projected = jnp.dot(
        gathered,
        lax.all_gather(w_qkv, ("dp", "fsdp"), axis=0, tiled=True),
        preferred_element_type=jnp.float32,
    )
    narrow_rank_rows = a_query.shape[1]
    down_projected = jnp.dot(
        gathered, jnp.concatenate([a_query, a_value], 1), preferred_element_type=jnp.float32
    ).astype(jnp.bfloat16)
    kv_local = col_count // ((QUERY_PER_KV + 2) * HD)
    grouped_queries = projected.reshape(sequence_length, kv_local, QUERY_PER_KV + 2, HD)
    query_rows = (
        grouped_queries[:, :, :QUERY_PER_KV].reshape(sequence_length, -1)
        + ADAPTER_SCALE
        * jnp.dot(
            down_projected[:, :narrow_rank_rows],
            query_up_adapter,
            preferred_element_type=jnp.float32,
        )
    ).astype(jnp.bfloat16)
    key_heads = (
        grouped_queries[:, :, QUERY_PER_KV].reshape(sequence_length, -1).astype(jnp.bfloat16)
    )
    value_rows = (
        grouped_queries[:, :, QUERY_PER_KV + 1].reshape(sequence_length, -1)
        + ADAPTER_SCALE
        * jnp.dot(
            down_projected[:, narrow_rank_rows:],
            value_up_adapter,
            preferred_element_type=jnp.float32,
        )
    ).astype(jnp.bfloat16)
    grad_rows = lax.all_to_all(out_grad[0], "tensor", split_axis=1, concat_axis=0, tiled=True)
    attended, pullback = jax.vjp(attend, query_rows, key_heads, value_rows)
    query_gradient, grad_keys, value_gradient = pullback(grad_rows)
    out_rows = lax.all_to_all(attended, "tensor", split_axis=0, concat_axis=1, tiled=True)
    query_up_gradient = ADAPTER_SCALE * jnp.einsum(
        "fb,fd->bd",
        down_projected[:, :narrow_rank_rows],
        query_gradient,
        preferred_element_type=jnp.float32,
    )
    value_up_gradient = ADAPTER_SCALE * jnp.einsum(
        "fb,fd->bd",
        down_projected[:, narrow_rank_rows:],
        value_gradient,
        preferred_element_type=jnp.float32,
    )
    middle_gradient = jnp.concatenate(
        [
            jnp.dot(query_gradient, query_up_adapter.T, preferred_element_type=jnp.float32),
            jnp.dot(value_gradient, value_up_adapter.T, preferred_element_type=jnp.float32),
        ],
        1,
    )
    mid_summed = lax.psum(middle_gradient, "tensor").astype(jnp.bfloat16)
    down_gradient = ADAPTER_SCALE * jnp.einsum(
        "uh,ux->hx", gathered, mid_summed, preferred_element_type=jnp.float32
    )
    down_gradient, query_up_gradient, value_up_gradient = lax.psum(
        (down_gradient, query_up_gradient, value_up_gradient), ("dp", "fsdp")
    )
    return (
        out_rows[None],
        down_gradient[:, :narrow_rank_rows],
        query_up_gradient,
        down_gradient[:, narrow_rank_rows:],
        value_up_gradient,
    )


def solution(mesh):
    return jax.shard_map(
        local,
        mesh=mesh,
        in_specs=(
            P(("dp", "fsdp"), "tensor", None),
            P(),
            P(("dp", "fsdp"), "tensor"),
            P(),
            P(None, "tensor"),
            P(),
            P(None, "tensor"),
            P(("dp", "fsdp"), "tensor", None),
        ),
        out_specs=(
            P(("dp", "fsdp"), "tensor", None),
            P(),
            P(None, "tensor"),
            P(),
            P(None, "tensor"),
        ),
        check_vma=False,
    )
```

profile of v0, /device:TPU:0, one launch (start us, length us, event | category | flops | bytes accessed | tf_op | source)
XLA Modules:
  0.0 691.3 jit_solution(7818503089707505698)
XLA Ops:
  7.2 2.8 fusion.62
  10.0 3.3 fusion.64
  17.5 6.3 all-to-all-start.1
  25.4 77.7 %all-to-all-done.1 = bf16[192,4,1024]{2,0,1:T(8,128)(2,1)S(1)} async-done(((bf16[192,4,1024]{2,0,1:T(8,128)(2,1)}), bf16[192,4,1024]{2,0,1:T(8,128)(2,1)S(1)}, u32[]{:S(2)}, u32[]{:S(2)}) %all-to-all-start.1) | async-done | bytes 1572896 | tf_op jit(solution)/shard_map/all_to_all | solution.py:106
  105.0 158.8 %all-gather.3.cloned.1.call-done = bf16[768,8192]{1,0:T(8,128)(2,1)} async-done(((bf16[192,8192]{1,0:T(8,128)(2,1)}), bf16[768,8192]{1,0:T(8,128)(2,1)}) %all-gather.3.cloned.1.call-update) | async-done | bytes 12582928 | tf_op jit(solution)/shard_map/all_gather | solution.py:71
  263.8 8.4 %convolution_convert_fusion.2 = bf16[768,32]{0,1:T(8,128)(2,1)S(1)} fusion(bf16[768,8192]{1,0:T(8,128)(2,1)} %all-gather.3.cloned.1.call-done, bf16[8192,16]{0,1:T(8,128)(2,1)S(1)} %copy-done.6, bf16[8192,16]{0,1:T(8,128)(2,1)S(1)} %copy-done.7), kind=kOutput, calls=%fused_computation.94 | convolution fusion | flops 403726336 | bytes 13156352 | tf_op jit(solution)/shard_map/dot_general | solution.py:80
  272.2 100.1 %all-gather.5.cloned.1.call-done = bf16[8192,1280]{1,0:T(8,128)(2,1)} async-done(((bf16[1024,1280]{1,0:T(8,128)(2,1)}), bf16[8192,1280]{1,0:T(8,128)(2,1)}) %all-gather.5.cloned.1.call-update) | async-done | bytes 20971536 | tf_op jit(solution)/shard_map/all_gather | solution.py:76
  372.3 22.9 %fusion.95 = f32[768,1280]{0,1:T(8,128)S(1)} fusion(bf16[768,8192]{1,0:T(8,128)(2,1)} %all-gather.3.cloned.1.call-done, bf16[8192,1280]{1,0:T(8,128)(2,1)} %all-gather.5.cloned.1.call-done), kind=kOutput, calls=%fused_computation.131 | convolution fusion | flops 16106127360 | bytes 37486592 | tf_op jit(solution)/shard_map/dot_general | solution.py:74
  399.3 2.5 add_convert_fusion
  407.8 85.5 %while.52 = (s32[]{:T(128)}, bf16[8,768,128]{2,1,0:T(8,128)(2,1)}, s32[8]{0:T(128)S(1)}, bf16[8,128,768]{2,1,0:T(8,128)(2,1)}, f32[8,768,768]{1,2,0:T(8,128)}, /...) while((s32[]{:T(128)}, bf16[8,768,128]{2,1,0:T(8,128)(2,1)}, ...), condition=%wide.region_5.6_spmd.clone, body=%wide.region_1.5_spmd.clone.sunk | while | flops 310344960 | bytes 20494060 | solution.py:65
  411.8 2.5 fusion.126
  422.4 2.5 fusion.126
  433.1 2.5 fusion.126
  443.7 2.6 fusion.126
  454.4 2.6 fusion.126
  465.1 2.6 fusion.126
  475.8 2.5 fusion.126
  486.5 2.5 fusion.126
  493.5 98.7 %while.53 = (s32[]{:T(128)}, bf16[768,8,128]{0,2,1:T(8,128)(2,1)S(1)}, bf16[768,1,128]{2,0,1:T(8,128)(2,1)}, s32[8]{0:T(128)S(1)}, bf16[8,768,128]{2,1,0:T(8,128...) while((s32[]{:T(128)}, ...), condition=%wide.region_9.10_spmd.clone, body=%wide.region_6.9_spmd.clone.sunk | while | flops 464683776 | bytes 17364168 | solution.py:65
  499.7 3.0 fusion.133
  503.5 2.4 fusion.134
  506.0 2.4 fusion.131
  511.9 3.0 fusion.133
  515.8 2.5 fusion.134
  518.3 2.4 fusion.131
  524.3 3.0 fusion.133
  528.1 2.5 fusion.134
  530.6 2.4 fusion.131
  536.6 3.0 fusion.133
  540.4 2.5 fusion.134
  543.0 2.4 fusion.131
  548.9 3.0 fusion.133
  552.7 2.5 fusion.134
  555.3 2.4 fusion.131
  561.2 3.0 fusion.133
  565.1 2.5 fusion.134
  567.6 2.4 fusion.131
  573.5 3.0 fusion.133
  577.4 2.5 fusion.134
  579.9 2.4 fusion.131
  585.9 3.0 fusion.133
  589.7 2.5 fusion.134
  595.4 20.2 %psum.28 = bf16[768,32]{0,1:T(8,128)(2,1)S(1)} all-reduce(f32[768,32]{0,1:T(8,128)S(1)} %pad_maximum_fusion.2), channel_id=1, replica_groups=mesh['dp'=4,'fsdp'=2,'tensor'=4] {'tensor'}, use_global_device_ids=true, to_apply=%region_10.11 | all-reduce | flops 24576 | bytes 147456 | tf_op jit(solution)/shard_map/psum | solution.py:129
  615.6 7.9 %convolution_multiply_fusion = f32[8192,32]{0,1:T(8,128)} fusion(bf16[768,8192]{1,0:T(8,128)(2,1)} %all-gather.3.cloned.1.call-done, bf16[768,32]{0,1:T(8,128)(2,1)S(1)} %psum.28), kind=kOutput, calls=%fused_computation.71 | convolution fusion | flops 402915328 | bytes 13680640 | tf_op jit(solution)/shard_map/uh,ux->hx/dot_general | solution.py:130
  626.7 3.6 all-to-all-start
  630.4 13.6 %psum.31 = f32[16,128]{1,0:T(8,128)} all-reduce(f32[16,128]{1,0:T(8,128)S(1)} %convolution_multiply_fusion.3), channel_id=1, replica_groups=mesh['dp'=4,'fsdp'=2,'tensor'=4] {'dp','fsdp'}, use_global_device_ids=true, to_apply=%region_13.14 | all-reduce | flops 2048 | bytes 16384 | tf_op jit(solution)/shard_map/psum | solution.py:133
  644.0 34.3 %all-reduce.5.cloned.1.call-done = (f32[8192,32]{0,1:T(8,128)}, f32[16,1024]{1,0:T(8,128)}) async-done(((f32[8192,32]{0,1:T(8,128)}, f32[16,1024]{1,0:T(8,128)}), (f32[8192,32]{0,1:T(8,128)}, f32[16,1024]{1,0:T(8,128)})) %all-reduce.5.cloned.1.call-update) | async-done | bytes 1114128 | tf_op jit(solution)/shard_map/psum | solution.py:133
  681.7 2.4 broadcast_in_dim.200
  (240 shorter events, 115.1 us)
Async XLA Ops:
  7.2 392.2 %copy-start = (bf16[16,1024]{1,0:T(8,128)(2,1)S(1)}, bf16[16,1024]{1,0:T(8,128)(2,1)}, u32[]{:S(2)}) copy-start(bf16[16,1024]{1,0:T(8,128)(2,1)} %param.16) | copy-start | bytes 98308
  7.2 2.8 copy-start.1
  7.2 256.6 %all-gather.3.cloned.1.call-start = ((), (), s32[]{:S(2)}) async-start(), calls=%async_computation.2 | async-start | bytes 15728640 | tf_op jit(solution)/shard_map/all_gather | solution.py:71
  13.3 1.4 copy-start.3
  13.3 359.0 %all-gather.5.cloned.1.call-start = ((), (), s32[]{:S(2)}) async-start(), calls=%async_computation.3 | async-start | bytes 23592960 | tf_op jit(solution)/shard_map/all_gather | solution.py:76
  17.5 85.6 %all-to-all-start.1 = ((bf16[192,4,1024]{2,0,1:T(8,128)(2,1)}), bf16[192,4,1024]{2,0,1:T(8,128)(2,1)S(1)}, u32[]{:S(2)}, u32[]{:S(2)}) async-start(bf16[192,4,1024]{2,0,1:T(8,128)(2,1)} %copy.38), calls=%async_computation.1 | async-start | bytes 3145728 | tf_op jit(solution)/shard_map/all_to_all | solution.py:106
  23.9 654.4 %all-reduce.5.cloned.1.call-start = ((), (), s32[]{:S(2)}) async-start(), calls=%async_computation.4 | async-start | bytes 2228224 | tf_op jit(solution)/shard_map/psum | solution.py:133
  103.6 160.3 %copy-start.6 = (bf16[8192,16]{0,1:T(8,128)(2,1)S(1)}, bf16[8192,16]{0,1:T(8,128)(2,1)}, u32[]{:S(2)}) copy-start(bf16[8192,16]{0,1:T(8,128)(2,1)} %param.17) | copy-start | bytes 786436
  103.6 160.2 %copy-start.7 = (bf16[8192,16]{0,1:T(8,128)(2,1)S(1)}, bf16[8192,16]{0,1:T(8,128)(2,1)}, u32[]{:S(2)}) copy-start(bf16[8192,16]{0,1:T(8,128)(2,1)} %param.15) | copy-start | bytes 786436
  406.9 0.7 copy-start.9
  592.2 0.9 copy-start.2
  593.7 1.5 copy-start.5
  615.6 8.0 %copy-start.4 = (bf16[8,768,128]{2,1,0:T(8,128)(2,1)S(1)}, bf16[8,768,128]{2,1,0:T(8,128)(2,1)}, u32[]{:S(2)}) copy-start(bf16[8,768,128]{2,1,0:T(8,128)(2,1)} %get-tuple-element.648) | copy-start | bytes 4718596
  626.7 53.8 %all-to-all-start = ((bf16[4,192,1024]{2,1,0:T(8,128)(2,1)}), bf16[4,192,1024]{2,1,0:T(8,128)(2,1)S(1)}, u32[]{:S(2)}, u32[]{:S(2)}) async-start(bf16[4,192,1024]{2,1,0:T(8,128)(2,1)} %all_to_all.24), calls=%async_computation | async-start | bytes 3145728 | tf_op jit(solution)/shard_map/all_to_all | solution.py:109
  681.7 2.4 copy-start.8
Sparse Core Ops, SparseCore 0:
  13.4 250.3 all-gather.2
  265.7 106.5 all-gather.4
  623.7 54.5 all-reduce.4
where the time goes:
time: 693 us; the launch traced here: 691 us
  waiting for transfers between devices  372 us (54%)
  matrix products  121 us (17%)
  other arithmetic  66.7 us (10%)
  local copies, waits for them, and re-layouts  57.7 us (8%)
  blocking collectives  33.8 us (5%)
  loops' own time  16.5 us (2%)
  between operations  14.1 us (2%)
  starting transfers between devices  9.99 us (1%)
    all_gather x1, waiting for transfers between devices, local(): gathered = lax.all_gather(normed_input, 'tensor', axis=0, tiled=True)  159 us
    all_gather x1, waiting for transfers between devices, local(): lax.all_gather(w_qkv, ('dp', 'fsdp'), axis=0, tiled=True)  100 us
    all_to_all x1, waiting for transfers between devices, local(): lax.all_to_all(out_grad[0], 'tensor', split_axis=1, concat_axis=0, tiled=...  77.7 us
    dot_general x24, matrix products, one_head(): jnp.dot(probabilities, v_head, preferred_element_type=jnp.float32)  48.5 us
    psum x1, waiting for transfers between devices, local(): lax.psum((down_gradient, query_up_gradient, value_up_gradient), ('dp', 'f...  34.3 us
    dynamic_update_slice x24, other arithmetic, attend(): lax.map(one_head, jnp.arange(kv_heads * QUERY_PER_KV, dtype=jnp.int32))  31.9 us
    dot_general x16, matrix products, one_head(): jnp.dot(q_head, k_head.T, preferred_element_type=jnp.float32)  28.8 us
    dot_general x1, matrix products, local(): jnp.dot(gathered, lax.all_gather(w_qkv, ('dp', 'fsdp'), axis=0, tiled=Tru...  22.9 us
  transfers between devices with their start and end apart: 5, of which 4 were waited for; matrix products, arithmetic and copies ran while one was open for 2% of the time, Pallas kernels for 0%

commit v1 on v0

--- a/solution.py
+++ b/solution.py
@@ -68,7 +68,14 @@
 
 def local(tokens, norm_gain, w_qkv, a_query, query_up_adapter, a_value, value_up_adapter, out_grad):
     normed_input = normalize(tokens[0], norm_gain)
-    gathered = lax.all_gather(normed_input, "tensor", axis=0, tiled=True)
+    ring = [normed_input]
+    for hop in range(3):
+        ring.append(lax.ppermute(ring[-1], "tensor", [(dev, (dev + 1) % 4) for dev in range(4)]))
+    gathered = jnp.roll(
+        jnp.concatenate(ring[::-1], axis=0),
+        (lax.axis_index("tensor") + 1) * ring[0].shape[0],
+        axis=0,
+    )
     sequence_length = gathered.shape[0]
     col_count = w_qkv.shape[1]
     projected = jnp.dot(

time: 693 us -> 624 us (0.900)
  waiting for transfers between devices: 372 us -> 268 us
  local copies, waits for them, and re-layouts: 57.7 us -> 88.6 us
    all_gather x1 -> x0, waiting for transfers between devices: 159 us -> none  [local(): gathered = lax.all_gather(normed_input, 'tensor', axis=0, tiled=True)]
    ppermute x0 -> x3, waiting for transfers between devices: none -> 141 us  [local(): lax.ppermute(ring[-1], 'tensor', [(dev, (dev + 1) % 4) for dev in range(4)])]
    all_gather x1, waiting for transfers between devices: 100 us -> 0.02 us  [local(): lax.all_gather(w_qkv, ('dp', 'fsdp'), axis=0, tiled=True)]
    unnamed x24 -> x38, local copies, waits for them, and re-layouts: 5.55 us -> 26 us
    all_to_all x1, waiting for transfers between devices: 77.7 us -> 90.7 us  [local(): lax.all_to_all(out_grad[0], 'tensor', split_axis=1, concat_axis=0, tiled=...]
  transfers between devices with their start and end apart: 5 -> 7, of which waited for: 4 -> 4; matrix products, arithmetic and copies ran while one was open for 2% -> 5% of each run, Pallas kernels for 0% -> 0%
where the time goes in v1:
time: 624 us; the launch traced here: 622 us
  waiting for transfers between devices  268 us (43%)
  matrix products  120 us (19%)
  local copies, waits for them, and re-layouts  88.6 us (14%)
  other arithmetic  70.8 us (11%)
  blocking collectives  31.4 us (5%)
  loops' own time  16.5 us (3%)
  between operations  14.5 us (2%)
  starting transfers between devices  11.8 us (2%)
    ppermute x3, waiting for transfers between devices, local(): lax.ppermute(ring[-1], 'tensor', [(dev, (dev + 1) % 4) for dev in range(4)])  141 us
    all_to_all x1, waiting for transfers between devices, local(): lax.all_to_all(out_grad[0], 'tensor', split_axis=1, concat_axis=0, tiled=...  90.7 us
    dot_general x24, matrix products, one_head(): jnp.dot(probabilities, v_head, preferred_element_type=jnp.float32)  48.7 us
    dynamic_update_slice x24, other arithmetic, attend(): lax.map(one_head, jnp.arange(kv_heads * QUERY_PER_KV, dtype=jnp.int32))  36.6 us
    psum x1, waiting for transfers between devices, local(): lax.psum((down_gradient, query_up_gradient, value_up_gradient), ('dp', 'f...  35.4 us
    dot_general x16, matrix products, one_head(): jnp.dot(q_head, k_head.T, preferred_element_type=jnp.float32)  28.8 us
    unnamed x38, local copies, waits for them, and re-layouts  26 us
    dot_general x1, matrix products, local(): jnp.dot(gathered, lax.all_gather(w_qkv, ('dp', 'fsdp'), axis=0, tiled=Tru...  23.2 us
  transfers between devices with their start and end apart: 7, of which 4 were waited for; matrix products, arithmetic and copies ran while one was open for 5% of the time, Pallas kernels for 0%

profile of v1, /device:TPU:0, one launch (start us, length us, event | category | flops | bytes accessed | tf_op | source)
XLA Modules:
  0.0 622.2 jit_solution(341606417384879904)
XLA Ops:
  7.9 2.8 fusion.71
  11.6 3.1 collective-permute-start
  14.7 70.1 %collective-permute-done = bf16[192,8192]{1,0:T(8,128)(2,1)S(1)} collective-permute-done((bf16[192,8192]{1,0:T(8,128)(2,1)S(1)}, bf16[192,8192]{1,0:T(8,128)(2,1)S(1)}, u32[]{:S(2)}, u32[]{:S(2)}) %collective-permute-start) | collective-permute-done | bytes 3145760 | tf_op jit(solution)/shard_map/ppermute | solution.py:73
  86.6 71.2 %collective-permute-done.1 = bf16[192,8192]{1,0:T(8,128)(2,1)} collective-permute-done((bf16[192,8192]{1,0:T(8,128)(2,1)S(1)}, bf16[192,8192]{1,0:T(8,128)(2,1)}, u32[]{:S(2)}, u32[]{:S(2)}) %collective-permute-start.1) | collective-permute-done | bytes 3145760 | tf_op jit(solution)/shard_map/ppermute | solution.py:73
  157.7 3.9 all_to_all.27
  161.6 3.0 copy.38
  164.6 5.1 all-to-all-start.1
  171.3 90.7 %all-to-all-done.1 = bf16[192,4,1024]{2,0,1:T(8,128)(2,1)} async-done(((bf16[192,4,1024]{2,0,1:T(8,128)(2,1)}), bf16[192,4,1024]{2,0,1:T(8,128)(2,1)}, u32[]{:S(2)}, u32[]{:S(2)}) %all-to-all-start.1) | async-done | bytes 1572896 | tf_op jit(solution)/shard_map/all_to_all | solution.py:113
  276.8 8.3 %copy-done.2 = bf16[1536,8192]{1,0:T(8,128)(2,1)} copy-done((bf16[1536,8192]{1,0:T(8,128)(2,1)}, bf16[1536,8192]{1,0:T(8,128)(2,1)S(1)}, u32[]{:S(2)}) %copy-start.2) | copy-done | bytes 25165848
  285.1 4.8 fusion.81
  290.0 23.2 %fusion.66 = f32[768,1280]{0,1:T(8,128)S(1)} fusion(bf16[8192,1280]{1,0:T(8,128)(2,1)} %all-gather.2.cloned.1.call-done, bf16[1536,8192]{1,0:T(8,128)(2,1)} %copy-done.2, s32[]{:T(128)S(6)} %select_n.67), kind=kOutput, calls=%fused_computation.75 | convolution fusion | flops 16106127360 | bytes 37486596 | tf_op jit(solution)/shard_map/dot_general | solution.py:81
  316.9 2.4 fusion.88
  319.3 2.4 copy.43
  321.8 3.7 add_convert_fusion
  328.2 90.0 %while.52 = (s32[]{:T(128)}, bf16[8,768,128]{2,1,0:T(8,128)(2,1)}, s32[8]{0:T(128)S(1)}, bf16[8,128,768]{2,1,0:T(8,128)(2,1)}, f32[8,768,768]{1,2,0:T(8,128)}, /...) while((s32[]{:T(128)}, bf16[8,768,128]{2,1,0:T(8,128)(2,1)}, ...), condition=%wide.region_5.6_spmd.clone, body=%wide.region_1.5_spmd.clone.sunk | while | flops 310344960 | bytes 20493544 | solution.py:65
  332.1 2.6 fusion.137
  343.4 2.6 fusion.137
  354.6 2.5 fusion.137
  365.8 2.5 fusion.137
  377.0 2.6 fusion.137
  388.3 2.5 fusion.137
  399.5 2.6 fusion.137
  410.8 2.6 fusion.137
  418.3 104.3 %while.53 = (s32[]{:T(128)}, bf16[768,8,128]{0,2,1:T(8,128)(2,1)S(1)}, bf16[768,1,128]{2,0,1:T(8,128)(2,1)}, s32[8]{0:T(128)S(1)}, bf16[8,768,128]{2,1,0:T(8,128...) while((s32[]{:T(128)}, ...), condition=%wide.region_9.10_spmd.clone, body=%wide.region_6.9_spmd.clone.sunk | while | flops 464683776 | bytes 17364168 | solution.py:65
  425.2 3.0 fusion.144
  429.1 2.5 fusion.145
  432.2 2.4 fusion.142
  438.2 3.0 fusion.144
  442.0 2.5 fusion.145
  445.3 2.4 fusion.142
  451.2 3.0 fusion.144
  455.1 2.5 fusion.145
  464.2 3.0 fusion.144
  468.1 2.5 fusion.145
  477.3 3.0 fusion.144
  481.1 2.5 fusion.145
  490.3 3.0 fusion.144
  494.1 2.5 fusion.145
  503.3 3.0 fusion.144
  507.1 2.5 fusion.145
  516.3 3.0 fusion.144
  520.2 2.5 fusion.145
  525.9 17.2 %psum.28 = bf16[768,32]{0,1:T(8,128)(2,1)S(1)} all-reduce(f32[768,32]{0,1:T(8,128)S(1)} %pad_maximum_fusion.2), channel_id=1, replica_groups=mesh['dp'=4,'fsdp'=2,'tensor'=4] {'tensor'}, use_global_device_ids=true, to_apply=%region_10.11 | all-reduce | flops 24576 | bytes 147456 | tf_op jit(solution)/shard_map/psum | solution.py:136
  543.1 9.3 %fusion.68 = f32[8192,32]{0,1:T(8,128)} fusion(bf16[1536,8192]{1,0:T(8,128)(2,1)} %copy-done.2, s32[]{:T(128)S(6)} %select_n.67, bf16[768,32]{0,1:T(8,128)(2,1)S(1)} %psum.28), kind=kOutput, calls=%fused_computation.77 | convolution fusion | flops 402915328 | bytes 13680644 | tf_op jit(solution)/shard_map/uh,ux->hx/dot_general | solution.py:137
  555.5 3.6 all-to-all-start
  559.2 14.2 %psum.31 = f32[16,128]{1,0:T(8,128)} all-reduce(f32[16,128]{1,0:T(8,128)S(1)} %convolution_multiply_fusion.2), channel_id=1, replica_groups=mesh['dp'=4,'fsdp'=2,'tensor'=4] {'dp','fsdp'}, use_global_device_ids=true, to_apply=%region_13.14 | all-reduce | flops 2048 | bytes 16384 | tf_op jit(solution)/shard_map/psum | solution.py:140
  573.4 35.4 %all-reduce.5.cloned.1.call-done = (f32[8192,32]{0,1:T(8,128)}, f32[16,1024]{1,0:T(8,128)}) async-done(((f32[8192,32]{0,1:T(8,128)}, f32[16,1024]{1,0:T(8,128)}), (f32[8192,32]{0,1:T(8,128)}, f32[16,1024]{1,0:T(8,128)})) %all-reduce.5.cloned.1.call-update) | async-done | bytes 1114128 | tf_op jit(solution)/shard_map/psum | solution.py:140
  612.3 2.4 broadcast_in_dim.200
  (259 shorter events, 145.0 us)
Async XLA Ops:
  7.2 314.6 %copy-start = (bf16[16,1024]{1,0:T(8,128)(2,1)S(1)}, bf16[16,1024]{1,0:T(8,128)(2,1)}, u32[]{:S(2)}) copy-start(bf16[16,1024]{1,0:T(8,128)(2,1)} %param.16) | copy-start | bytes 98308
  7.2 3.6 copy-start.1
  7.2 3.6 copy-start.11
  7.2 282.8 %all-gather.2.cloned.1.call-start = ((), (), s32[]{:S(2)}) async-start(), calls=%async_computation.2 | async-start | bytes 23592960 | tf_op jit(solution)/shard_map/all_gather | solution.py:83
  11.6 73.2 %collective-permute-start = (bf16[192,8192]{1,0:T(8,128)(2,1)S(1)}, bf16[192,8192]{1,0:T(8,128)(2,1)S(1)}, u32[]{:S(2)}, u32[]{:S(2)}) collective-permute-start(bf16[192,8192]{1,0:T(8,128)(2,1)S(1)} %fusion.73), channel_id=1, source_target_pairs={{0,1},{1,2},{2,3},{3,0},{4,5},{5,6},{6,7},{7,4},{8,9},{9,10},{10,1... | collective-permute-start | bytes 9437192 | tf_op jit(solution)/shard_map/ppermute | solution.py:73
  84.9 1.7 copy-start.3
  86.6 71.2 %collective-permute-start.1 = (bf16[192,8192]{1,0:T(8,128)(2,1)S(1)}, bf16[192,8192]{1,0:T(8,128)(2,1)}, u32[]{:S(2)}, u32[]{:S(2)}) collective-permute-start(bf16[192,8192]{1,0:T(8,128)(2,1)S(1)} %collective-permute-done), channel_id=1, source_target_pairs={{0,1},{1,2},{2,3},{3,0},{4,5},{5,6},{6,7},{7,4},{8,9},{9,10},{10,1... | collective-permute-start | bytes 9437192 | tf_op jit(solution)/shard_map/ppermute | solution.py:73
  157.7 107.5 %collective-permute-start.2 = (bf16[192,8192]{1,0:T(8,128)(2,1)}, bf16[192,8192]{1,0:T(8,128)(2,1)}, u32[]{:S(2)}, u32[]{:S(2)}) collective-permute-start(bf16[192,8192]{1,0:T(8,128)(2,1)} %collective-permute-done.1), channel_id=1, source_target_pairs={{0,1},{1,2},{2,3},{3,0},{4,5},{5,6},{6,7},{7,4},{8,9},{9,10},{10,1... | collective-permute-start | bytes 9437192 | tf_op jit(solution)/shard_map/ppermute | solution.py:73
  164.6 97.3 %all-to-all-start.1 = ((bf16[192,4,1024]{2,0,1:T(8,128)(2,1)}), bf16[192,4,1024]{2,0,1:T(8,128)(2,1)}, u32[]{:S(2)}, u32[]{:S(2)}) async-start(bf16[192,4,1024]{2,0,1:T(8,128)(2,1)} %copy.38), calls=%async_computation.1 | async-start | bytes 3145728 | tf_op jit(solution)/shard_map/all_to_all | solution.py:113
  169.7 439.2 %all-reduce.5.cloned.1.call-start = ((), (), s32[]{:S(2)}) async-start(), calls=%async_computation.3 | async-start | bytes 2228224 | tf_op jit(solution)/shard_map/psum | solution.py:140
  267.3 2.8 copy-start.4
  276.8 8.3 %copy-start.2 = (bf16[1536,8192]{1,0:T(8,128)(2,1)}, bf16[1536,8192]{1,0:T(8,128)(2,1)S(1)}, u32[]{:S(2)}) copy-start(bf16[1536,8192]{1,0:T(8,128)(2,1)S(1)} %constant_dynamic-update-slice_fusion.1) | copy-start | bytes 75497472
  325.5 1.8 copy-start.8
  325.5 1.8 copy-start.13
  325.5 2.1 copy-start.10
  325.5 2.1 copy-start.5
  522.7 0.9 copy-start.6
  524.2 1.5 copy-start.9
  543.1 9.3 %copy-start.7 = (bf16[8,768,128]{2,1,0:T(8,128)(2,1)S(1)}, bf16[8,768,128]{2,1,0:T(8,128)(2,1)}, u32[]{:S(2)}) copy-start(bf16[8,768,128]{2,1,0:T(8,128)(2,1)} %get-tuple-element.648) | copy-start | bytes 4718596
  555.5 55.6 %all-to-all-start = ((bf16[4,192,1024]{2,1,0:T(8,128)(2,1)}), bf16[4,192,1024]{2,1,0:T(8,128)(2,1)S(1)}, u32[]{:S(2)}, u32[]{:S(2)}) async-start(bf16[4,192,1024]{2,1,0:T(8,128)(2,1)} %all_to_all.24), calls=%async_computation | async-start | bytes 3145728 | tf_op jit(solution)/shard_map/all_to_all | solution.py:116
  612.3 2.4 copy-start.12
Sparse Core Ops, SparseCore 0:
  9.9 110.1 all-gather.1
  552.5 56.2 all-reduce.4
